TPU v7x, 32 devices: a whole 2x2x4 slice. The times are simulated.
32 devices in a mesh: ex: 8 (over y, x, core), tp: 4 (over z).
Axes of the slice: x: 2, y: 2, z: 4, core: 2. Of those that a mesh axis runs over, the one named last changes fastest.
Arguments:
- samples: bfloat16 [192, 2048], P(('ex', 'tp')), may hold values from -6 to 6
- gate_weight: bfloat16 [2048, 44], replicated, may hold values from -15 to 15
- up_weight: bfloat16 [16, 2048, 4096], P('ex', None, 'tp'), may hold values from -0.125 to 0.125
- down_weight: bfloat16 [16, 4096, 2048], P('ex', 'tp'), may hold values from -0.09375 to 0.09375
Outputs:
- task_outputs: bfloat16 [192, 5, 2048], P(('ex', 'tp'))
All inputs are finite; a program needn't handle non-finite values.
Results may differ from a plain program's by a relative error of at most 0.0055.
Values may be sent and summed in bfloat16 or wider, within the bound.
A program may use at most 128 MiB of HBM per device.

v0:
```python
import jax
import jax.numpy as jnp
import numpy as np
from jax import lax
from jax.sharding import PartitionSpec as P

TASKS = 4
TASK_EXP = 3
SHARED = 4
EXPERTS = 16
GATES = 44


def routing_table():
    per_task = TASK_EXP + SHARED
    table = np.zeros((GATES, (TASKS + 1) * EXPERTS), np.float32)
    for task_idx in range(TASKS):
        for column in range(per_task):
            if column < TASK_EXP:
                expert_idx = task_idx * TASK_EXP + column
            else:
                expert_idx = TASKS * TASK_EXP + column - TASK_EXP
            table[task_idx * per_task + column, task_idx * EXPERTS + expert_idx] = 1.0
    for expert_idx in range(EXPERTS):
        table[TASKS * per_task + expert_idx, TASKS * EXPERTS + expert_idx] = 1.0
    return jnp.asarray(table, dtype=jnp.float32)


def gate_mix(rows, gate_weight):
    logits = jnp.dot(rows, gate_weight, preferred_element_type=jnp.float32)
    per_task = TASK_EXP + SHARED
    pieces = []
    for task_idx in range(TASKS):
        pieces.append(
            jax.nn.softmax(logits[:, task_idx * per_task : (task_idx + 1) * per_task], axis=-1)
        )
    pieces.append(jax.nn.softmax(logits[:, TASKS * per_task :], axis=-1))
    probs = jnp.concatenate(pieces, axis=1)
    mixed = jnp.dot(probs, routing_table(), precision=lax.Precision.HIGHEST)
    return mixed.reshape(rows.shape[0], TASKS + 1, EXPERTS)


def on_device(samples, gate_weight, up_weight, down_weight):
    local_experts = up_weight.shape[0]
    ex_count = lax.axis_size("ex")
    tp_count = lax.axis_size("tp")
    row_dev = samples.shape[0]
    width = samples.shape[1]
    piece = lax.all_gather(samples, ("ex", "tp"), axis=0, tiled=True)
    outputs = []
    for expert_idx in range(local_experts):
        outputs.append(
            jnp.maximum(
                jnp.dot(piece, up_weight[expert_idx], preferred_element_type=jnp.float32), 0.0
            ).astype(jnp.bfloat16)
        )
    hidden = jnp.stack(outputs, axis=1)
    partial_out = jnp.einsum(
        "rlf,lfd->rld", hidden, down_weight, preferred_element_type=jnp.float32
    )
    blocked = partial_out.reshape(ex_count, tp_count * row_dev, local_experts, width)
    summed = lax.psum_scatter(blocked, "tp", scatter_dimension=1, tiled=True)
    gathered = lax.all_to_all(summed, "ex", split_axis=0, concat_axis=2, tiled=True)[0]
    mixing = gate_mix(samples, gate_weight)
    result = jnp.einsum("rke,red->rkd", mixing, gathered, precision=lax.Precision.HIGHEST)
    return result.astype(jnp.bfloat16)


def solution(mesh):
    placed = (P(("ex", "tp"), None), P(), P("ex", None, "tp"), P("ex", "tp", None))
    return jax.shard_map(
        on_device,
        mesh=mesh,
        in_specs=placed,
        out_specs=P(("ex", "tp"), None, None),
        check_vma=False,
    )
```

profile of v0, /device:TPU:0, one launch (start us, length us, event | category | flops | bytes accessed | tf_op | source)
XLA Modules:
  0.0 185.9 jit_solution(10094937951658092538)
XLA Ops:
  6.5 78.9 %all-gather = bf16[32,6,2048]{2,1,0:T(8,128)(2,1)S(1)} all-gather(bf16[1,6,2048]{2,1,0:T(8,128)(2,1)} %bitcast.43), channel_id=1, replica_groups=mesh['ex'=8,'tp'=4] {'ex','tp'}, dimensions={0}, use_global_device_ids=true | all-gather | bytes 811008 | tf_op jit(solution)/shard_map/all_gather | solution.py:49
  85.5 0.3 reshape.20
  85.7 3.2 %fusion.21 = bf16[192,1,1024]{2,0,1:T(8,128)(2,1)S(1)} fusion(bf16[192,2048]{1,0:T(8,128)(2,1)S(1)} %reshape.20, bf16[2,2048,1024]{2,1,0:T(8,128)(2,1)} %param.7), kind=kOutput, calls=%fused_computation.12 | convolution fusion | flops 805699584 | bytes 5373952 | tf_op jit(solution)/shard_map/dot_general | solution.py:54
  88.9 3.2 %fusion.18 = bf16[192,1,1024]{2,0,1:T(8,128)(2,1)S(1)} fusion(bf16[192,2048]{1,0:T(8,128)(2,1)S(1)} %reshape.20, bf16[2,2048,1024]{2,1,0:T(8,128)(2,1)} %param.7), kind=kOutput, calls=%fused_computation.11 | convolution fusion | flops 805699584 | bytes 5373952 | tf_op jit(solution)/shard_map/dot_general | solution.py:54
  92.1 5.2 %fusion.24 = f32[2,192,2048]{2,1,0:T(8,128)S(1)} fusion(bf16[2,1024,2048]{2,1,0:T(8,128)(2,1)} %param.8, bf16[192,1,1024]{2,0,1:T(8,128)(2,1)S(1)} %fusion.21, bf16[192,1,1024]{2,0,1:T(8,128)(2,1)S(1)} %fusion.18), kind=kOutput, calls=%fused_computation.17 | convolution fusion | flops 1611005952 | bytes 12320768 | tf_op jit(solution)/shard_map/rlf,lfd->rld/dot_general | solution.py:58
  97.3 0.0 copy-start.1
  97.3 0.0 copy-start.5
  97.3 0.0 copy-start.6
  97.3 0.0 copy-start.4
  97.3 0.0 copy-start.3
  97.3 0.0 copy-start.2
  97.4 3.5 %copy.10 = f32[8,24,2,2048]{3,0,2,1:T(8,128)} copy(f32[8,24,2,2048]{3,1,0,2:T(8,128)S(1)} %bitcast.41) | data formatting | bytes 6291456 | tf_op jit(solution)/shard_map/reshape | solution.py:61
  100.8 0.0 reduce-scatter.2.cloned.1.call-update
  100.9 0.2 fusion.50
  101.0 0.2 slice_reduce_fusion
  101.2 0.2 slice_reduce_fusion.1
  101.5 0.2 fusion.37
  101.7 0.2 fusion.31
  101.9 0.2 convolution_add_fusion.3
  102.1 56.2 %reduce-scatter.2.cloned.1.call-done = f32[8,6,2,2048]{3,0,2,1:T(8,128)} async-done(((f32[8,24,2,2048]{3,0,2,1:T(8,128)}), f32[8,6,2,2048]{3,0,2,1:T(8,128)}) %reduce-scatter.2.cloned.1.call-update) | async-done | bytes 786448 | tf_op jit(solution)/shard_map/reduce_scatter | solution.py:62
  158.3 2.6 %copy.11 = f32[8,6,2,2048]{3,2,1,0:T(2,128)} copy(f32[8,6,2,2048]{3,0,2,1:T(8,128)} %reduce-scatter.2.cloned.1.call-done) | data formatting | bytes 1572864 | tf_op jit(solution)/shard_map/reduce_scatter | solution.py:62
  161.0 3.6 %all-to-all-start = ((f32[8,6,2,2048]{3,2,1,0:T(2,128)}), f32[8,6,2,2048]{3,2,1,0:T(2,128)S(1)}, u32[]{:S(2)}, u32[]{:S(2)}) async-start(f32[8,6,2,2048]{3,2,1,0:T(2,128)} %copy.11), calls=%async_computation.1 | async-start | bytes 1572864 | tf_op jit(solution)/shard_map/all_to_all | solution.py:63
  164.6 0.2 fusion.38
  164.8 0.2 convolution_add_fusion.2
  165.0 0.2 convolution_add_fusion.1
  165.2 0.2 convolution_add_fusion
  165.4 0.1 reshape.17
  165.5 11.7 %all-to-all-done = f32[8,6,2,2048]{3,2,1,0:T(2,128)S(1)} async-done(((f32[8,6,2,2048]{3,2,1,0:T(2,128)}), f32[8,6,2,2048]{3,2,1,0:T(2,128)S(1)}, u32[]{:S(2)}, u32[]{:S(2)}) %all-to-all-start) | async-done | bytes 786464 | tf_op jit(solution)/shard_map/all_to_all | solution.py:63
  177.2 0.1 copy.12
  177.2 0.5 squeeze.11
  177.8 0.5 convolution_convert_fusion
  178.3 0.8 copy.13
  (9 shorter events, 0.0 us)
Async XLA Ops:
  6.5 94.3 %copy-start = (bf16[2048,44]{0,1:T(8,128)(2,1)S(1)}, bf16[2048,44]{0,1:T(8,128)(2,1)}, u32[]{:S(2)}) copy-start(bf16[2048,44]{0,1:T(8,128)(2,1)} %param.6) | copy-start | bytes 540676
  6.5 151.8 %reduce-scatter.2.cloned.1.call-start = ((), (), s32[]{:S(2)}) async-start(), calls=%async_computation.2 | async-start | bytes 3932160 | tf_op jit(solution)/shard_map/reduce_scatter | solution.py:62
  97.3 3.6 %copy-start.1 = (bf16[6,2048]{1,0:T(8,128)(2,1)S(1)}, bf16[6,2048]{1,0:T(8,128)(2,1)}, u32[]{:S(2)}) copy-start(bf16[6,2048]{1,0:T(8,128)(2,1)} %param.5) | copy-start | bytes 73732
  97.3 4.4 %copy-start.5 = (f32[7,80]{1,0:T(8,128)S(1)}, f32[7,80]{1,0:T(8,128)}, u32[]{:S(2)}) copy-start(f32[7,80]{1,0:T(8,128)} %constant.12) | copy-start | bytes 6724
  97.3 4.6 %copy-start.6 = (f32[7,80]{1,0:T(8,128)S(1)}, f32[7,80]{1,0:T(8,128)}, u32[]{:S(2)}) copy-start(f32[7,80]{1,0:T(8,128)} %constant.13) | copy-start | bytes 6724
  97.3 67.5 %copy-start.4 = (f32[7,80]{1,0:T(8,128)S(1)}, f32[7,80]{1,0:T(8,128)}, u32[]{:S(2)}) copy-start(f32[7,80]{1,0:T(8,128)} %constant.14) | copy-start | bytes 6724
  97.3 67.7 %copy-start.3 = (f32[7,80]{1,0:T(8,128)S(1)}, f32[7,80]{1,0:T(8,128)}, u32[]{:S(2)}) copy-start(f32[7,80]{1,0:T(8,128)} %constant.15) | copy-start | bytes 6724
  97.3 67.9 %copy-start.2 = (f32[16,80]{1,0:T(8,128)S(1)}, f32[16,80]{1,0:T(8,128)}, u32[]{:S(2)}) copy-start(f32[16,80]{1,0:T(8,128)} %constant.16) | copy-start | bytes 15364
  161.0 16.2 %all-to-all-start = ((f32[8,6,2,2048]{3,2,1,0:T(2,128)}), f32[8,6,2,2048]{3,2,1,0:T(2,128)S(1)}, u32[]{:S(2)}, u32[]{:S(2)}) async-start(f32[8,6,2,2048]{3,2,1,0:T(2,128)} %copy.11), calls=%async_computation.1 | async-start | bytes 1572864 | tf_op jit(solution)/shard_map/all_to_all | solution.py:63
Sparse Core Ops, SparseCore 0:
  101.0 57.3 reduce-scatter.1
where the time goes:
time: 186 us
  blocking collectives  78.9 us (42%)
  waiting for transfers between devices  67.9 us (37%)
  between operations  13.5 us (7%)
  matrix products  13.2 us (7%)
  local copies, waits for them, and re-layouts  7.84 us (4%)
  starting transfers between devices  3.65 us (2%)
    all_gather x1, blocking collectives, on_device(): piece = lax.all_gather(samples, ('ex', 'tp'), axis=0, tiled=True)  78.9 us
    reduce_scatter x1, waiting for transfers between devices, on_device(): summed = lax.psum_scatter(blocked, 'tp', scatter_dimension=1, tiled=True)  56.2 us
    all_to_all x1, waiting for transfers between devices, on_device(): lax.all_to_all(summed, 'ex', split_axis=0, concat_axis=2, tiled=True)[0]  11.7 us
    dot_general x2, matrix products, on_device(): jnp.dot(piece, up_weight[expert_idx], preferred_element_type=jnp.float32)  6.35 us
    dot_general x1, matrix products, on_device(): jnp.einsum('rlf,lfd->rld', hidden, down_weight, preferred_element_type=jn...  5.18 us
  transfers between devices with their start and end apart: 2, of which 2 were waited for; matrix products, arithmetic and copies ran while one was open for 1% of the time, Pallas kernels for 0%

commit v1 on v0

--- a/solution.py
+++ b/solution.py
@@ -46,7 +46,11 @@
     tp_count = lax.axis_size("tp")
     row_dev = samples.shape[0]
     width = samples.shape[1]
-    piece = lax.all_gather(samples, ("ex", "tp"), axis=0, tiled=True)
+    peers = lax.axis_size(("ex", "tp"))
+    repeats = [peers if d == 0 else 1 for d in range(samples.ndim)]
+    piece = lax.all_to_all(
+        jnp.tile(samples, repeats), ("ex", "tp"), split_axis=0, concat_axis=0, tiled=True
+    )
     outputs = []
     for expert_idx in range(local_experts):
         outputs.append(

time: 186 us -> 143 us (0.77)
  blocking collectives: 78.9 us -> 32.1 us
  waiting for transfers between devices: 67.9 us -> 71 us
    all_gather x1 -> x0, blocking collectives: 78.9 us -> none  [on_device(): piece = lax.all_gather(samples, ('ex', 'tp'), axis=0, tiled=True)]
    all_to_all x0 -> x1, blocking collectives: none -> 32.1 us  [on_device(): lax.all_to_all(jnp.tile(samples, repeats), ('ex', 'tp'), split_axis=0, co...]
    reduce_scatter x1, waiting for transfers between devices: 56.2 us -> 59.3 us  [on_device(): summed = lax.psum_scatter(blocked, 'tp', scatter_dimension=1, tiled=True)]
where the time goes in v1:
time: 143 us
  waiting for transfers between devices  71 us (50%)
  blocking collectives  32.1 us (22%)
  between operations  13.5 us (9%)
  matrix products  13.2 us (9%)
  local copies, waits for them, and re-layouts  8.74 us (6%)
  starting transfers between devices  3.66 us (3%)
    reduce_scatter x1, waiting for transfers between devices, on_device(): summed = lax.psum_scatter(blocked, 'tp', scatter_dimension=1, tiled=True)  59.3 us
    all_to_all x1, blocking collectives, on_device(): lax.all_to_all(jnp.tile(samples, repeats), ('ex', 'tp'), split_axis=0, co...  32.1 us
    all_to_all x1, waiting for transfers between devices, on_device(): lax.all_to_all(summed, 'ex', split_axis=0, concat_axis=2, tiled=True)[0]  11.7 us
    dot_general x2, matrix products, on_device(): jnp.dot(piece, up_weight[expert_idx], preferred_element_type=jnp.float32)  6.35 us
    dot_general x1, matrix products, on_device(): jnp.einsum('rlf,lfd->rld', hidden, down_weight, preferred_element_type=jn...  5.18 us
    all_to_all x1, starting transfers between devices, on_device(): lax.all_to_all(summed, 'ex', split_axis=0, concat_axis=2, tiled=True)[0]  3.65 us
    reshape x1, local copies, waits for them, and re-layouts, on_device(): partial_out.reshape(ex_count, tp_count * row_dev, local_experts, width)  3.49 us
  transfers between devices with their start and end apart: 2, of which 2 were waited for; matrix products, arithmetic and copies ran while one was open for 1% of the time, Pallas kernels for 0%

profile of v1, /device:TPU:0, one launch (start us, length us, event | category | flops | bytes accessed | tf_op | source)
XLA Modules:
  0.0 143.1 jit_solution(15946620488880686702)
XLA Ops:
  6.5 0.9 tile.2
  7.5 32.1 %all_to_all.24 = bf16[32,6,2048]{2,1,0:T(8,128)(2,1)S(1)} all-to-all(bf16[32,6,2048]{2,1,0:T(8,128)(2,1)S(1)} %tile.2), channel_id=1, replica_groups=mesh['ex'=8,'tp'=4] {'ex','tp'}, dimensions={0} | all-to-all | bytes 1572864 | tf_op jit(solution)/shard_map/all_to_all | solution.py:51
  39.5 0.3 all_to_all.18
  39.8 3.2 %fusion.21 = bf16[192,1,1024]{2,0,1:T(8,128)(2,1)S(1)} fusion(bf16[192,2048]{1,0:T(8,128)(2,1)S(1)} %all_to_all.18, bf16[2,2048,1024]{2,1,0:T(8,128)(2,1)} %param.7), kind=kOutput, calls=%fused_computation.12 | convolution fusion | flops 805699584 | bytes 5373952 | tf_op jit(solution)/shard_map/dot_general | solution.py:58
  43.0 3.2 %fusion.18 = bf16[192,1,1024]{2,0,1:T(8,128)(2,1)S(1)} fusion(bf16[192,2048]{1,0:T(8,128)(2,1)S(1)} %all_to_all.18, bf16[2,2048,1024]{2,1,0:T(8,128)(2,1)} %param.7), kind=kOutput, calls=%fused_computation.11 | convolution fusion | flops 805699584 | bytes 5373952 | tf_op jit(solution)/shard_map/dot_general | solution.py:58
  46.1 5.2 %fusion.24 = f32[2,192,2048]{2,1,0:T(8,128)S(1)} fusion(bf16[2,1024,2048]{2,1,0:T(8,128)(2,1)} %param.8, bf16[192,1,1024]{2,0,1:T(8,128)(2,1)S(1)} %fusion.21, bf16[192,1,1024]{2,0,1:T(8,128)(2,1)S(1)} %fusion.18), kind=kOutput, calls=%fused_computation.17 | convolution fusion | flops 1611005952 | bytes 12320768 | tf_op jit(solution)/shard_map/rlf,lfd->rld/dot_general | solution.py:62
  51.3 0.0 copy-start.5
  51.4 0.0 copy-start.6
  51.4 0.0 copy-start.4
  51.4 0.0 copy-start.3
  51.4 0.0 copy-start.2
  51.4 3.5 %copy.10 = f32[8,24,2,2048]{3,0,2,1:T(8,128)} copy(f32[8,24,2,2048]{3,1,0,2:T(8,128)S(1)} %bitcast.40) | data formatting | bytes 6291456 | tf_op jit(solution)/shard_map/reshape | solution.py:65
  54.9 0.0 reduce-scatter.2.cloned.1.call-update
  54.9 0.2 fusion.50
  55.1 0.2 slice_reduce_fusion
  55.3 0.2 slice_reduce_fusion.1
  55.5 0.2 fusion.37
  55.8 0.2 fusion.31
  56.0 0.2 convolution_add_fusion.3
  56.2 59.3 %reduce-scatter.2.cloned.1.call-done = f32[8,6,2,2048]{3,0,2,1:T(8,128)} async-done(((f32[8,24,2,2048]{3,0,2,1:T(8,128)}), f32[8,6,2,2048]{3,0,2,1:T(8,128)}) %reduce-scatter.2.cloned.1.call-update) | async-done | bytes 786448 | tf_op jit(solution)/shard_map/reduce_scatter | solution.py:66
  115.5 2.6 %copy.11 = f32[8,6,2,2048]{3,2,1,0:T(2,128)} copy(f32[8,6,2,2048]{3,0,2,1:T(8,128)} %reduce-scatter.2.cloned.1.call-done) | data formatting | bytes 1572864 | tf_op jit(solution)/shard_map/reduce_scatter | solution.py:66
  118.1 3.7 %all-to-all-start.1 = ((f32[8,6,2,2048]{3,2,1,0:T(2,128)}), f32[8,6,2,2048]{3,2,1,0:T(2,128)S(1)}, u32[]{:S(2)}, u32[]{:S(2)}) async-start(f32[8,6,2,2048]{3,2,1,0:T(2,128)} %copy.11), calls=%async_computation.2 | async-start | bytes 1572864 | tf_op jit(solution)/shard_map/all_to_all | solution.py:67
  121.8 0.2 fusion.38
  122.0 0.2 convolution_add_fusion.2
  122.2 0.2 convolution_add_fusion.1
  122.4 0.2 convolution_add_fusion
  122.6 0.1 reshape.24
  122.7 11.7 %all-to-all-done.1 = f32[8,6,2,2048]{3,2,1,0:T(2,128)S(1)} async-done(((f32[8,6,2,2048]{3,2,1,0:T(2,128)}), f32[8,6,2,2048]{3,2,1,0:T(2,128)S(1)}, u32[]{:S(2)}, u32[]{:S(2)}) %all-to-all-start.1) | async-done | bytes 786464 | tf_op jit(solution)/shard_map/all_to_all | solution.py:67
  134.3 0.1 copy.12
  134.4 0.5 squeeze.11
  135.0 0.5 convolution_convert_fusion
  135.5 0.8 copy.13
  (10 shorter events, 0.0 us)
Async XLA Ops:
  6.5 48.4 %copy-start = (bf16[2048,44]{0,1:T(8,128)(2,1)S(1)}, bf16[2048,44]{0,1:T(8,128)(2,1)}, u32[]{:S(2)}) copy-start(bf16[2048,44]{0,1:T(8,128)(2,1)} %param.6) | copy-start | bytes 540676
  6.5 109.0 %reduce-scatter.2.cloned.1.call-start = ((), (), s32[]{:S(2)}) async-start(), calls=%async_computation.3 | async-start | bytes 3932160 | tf_op jit(solution)/shard_map/reduce_scatter | solution.py:66
  51.3 3.6 %copy-start.1 = (bf16[6,2048]{1,0:T(8,128)(2,1)S(1)}, bf16[6,2048]{1,0:T(8,128)(2,1)}, u32[]{:S(2)}) copy-start(bf16[6,2048]{1,0:T(8,128)(2,1)} %param.5) | copy-start | bytes 73732
  51.3 4.4 %copy-start.5 = (f32[7,80]{1,0:T(8,128)S(1)}, f32[7,80]{1,0:T(8,128)}, u32[]{:S(2)}) copy-start(f32[7,80]{1,0:T(8,128)} %constant.12) | copy-start | bytes 6724
  51.4 4.6 %copy-start.6 = (f32[7,80]{1,0:T(8,128)S(1)}, f32[7,80]{1,0:T(8,128)}, u32[]{:S(2)}) copy-start(f32[7,80]{1,0:T(8,128)} %constant.13) | copy-start | bytes 6724
  51.4 70.6 %copy-start.4 = (f32[7,80]{1,0:T(8,128)S(1)}, f32[7,80]{1,0:T(8,128)}, u32[]{:S(2)}) copy-start(f32[7,80]{1,0:T(8,128)} %constant.14) | copy-start | bytes 6724
  51.4 70.8 %copy-start.3 = (f32[7,80]{1,0:T(8,128)S(1)}, f32[7,80]{1,0:T(8,128)}, u32[]{:S(2)}) copy-start(f32[7,80]{1,0:T(8,128)} %constant.15) | copy-start | bytes 6724
  51.4 71.0 %copy-start.2 = (f32[16,80]{1,0:T(8,128)S(1)}, f32[16,80]{1,0:T(8,128)}, u32[]{:S(2)}) copy-start(f32[16,80]{1,0:T(8,128)} %constant.16) | copy-start | bytes 15364
  118.1 16.2 %all-to-all-start.1 = ((f32[8,6,2,2048]{3,2,1,0:T(2,128)}), f32[8,6,2,2048]{3,2,1,0:T(2,128)S(1)}, u32[]{:S(2)}, u32[]{:S(2)}) async-start(f32[8,6,2,2048]{3,2,1,0:T(2,128)} %copy.11), calls=%async_computation.2 | async-start | bytes 1572864 | tf_op jit(solution)/shard_map/all_to_all | solution.py:67
Sparse Core Ops, SparseCore 0:
  55.0 60.4 reduce-scatter.1
